TPU v7x, 32 devices: a whole 2x2x4 slice. The times are simulated.
32 devices in a mesh: seq: 8 (over z, x), res: 4 (over y, core).
Axes of the slice: x: 2, y: 2, z: 4, core: 2. Of those that a mesh axis runs over, the one named last changes fastest.
Arguments:
- alignment: bfloat16 [128, 4, 128, 256], P('seq', 'res'), may hold values from -8 to 8
- gain_attn: float32 [256], replicated, may hold values from 0.1 to 1.9
- w_proj: bfloat16 [256, 4, 256], replicated, may hold values from -0.75 to 0.75
- w_out: bfloat16 [256, 256], replicated, may hold values from -0.375 to 0.375
- gain_head: float32 [256], replicated, may hold values from 0.1 to 1.9
- w_head: bfloat16 [256, 23], replicated, may hold values from -1 to 1
- masked: int32 [128, 4, 128], P('res', None, 'seq'), may hold values from 0 to 1
- labels: int32 [128, 4, 128], P('res', None, 'seq'), may hold values from 0 to 22
Outputs:
- updated: bfloat16 [128, 4, 128, 256], P('res', None, 'seq')
- masked_loss: float32 [], replicated
- mask_share: float32 [], replicated
All inputs are finite; a program needn't handle non-finite values.
Results may differ from a plain program's by a relative error of at most 0.011.
Values may be sent and summed in bfloat16 or wider, within the bound.
A program may use at most 192 MiB of HBM per device.

v0:
```python
import jax
import jax.numpy as jnp
from jax import lax
from jax.sharding import PartitionSpec as P

HEADS = 8
HEAD_DIM = 32


def normalize(values, gain):
    mean = jnp.mean(values, axis=-1, keepdims=True)
    centred = values - mean
    spread = jnp.mean(centred * centred, axis=-1, keepdims=True)
    return centred * lax.rsqrt(spread + 1e-05) * gain


def project(flat_rows, gain_attn, w_proj):
    features = flat_rows.shape[1]
    normed = normalize(flat_rows.astype(jnp.float32), gain_attn).astype(jnp.bfloat16)
    return jnp.dot(
        normed, w_proj.reshape(features, 4 * features), preferred_element_type=jnp.float32
    ).astype(jnp.bfloat16)


def column_attention(queries, key_part, value_part):
    inv_root = HEAD_DIM ** (-0.5)
    scores = (
        jnp.einsum("shd,thd->hst", queries, key_part, preferred_element_type=jnp.float32) * inv_root
    )
    probs = jnp.exp(scores)
    totals = jnp.sum(probs, axis=2)
    weighted = jnp.einsum(
        "hst,thd->shd", probs.astype(jnp.bfloat16), value_part, preferred_element_type=jnp.float32
    )
    return (weighted, totals)


def finish(flat_rows, gated, w_out):
    summed = flat_rows.astype(jnp.float32) + jnp.dot(
        gated, w_out, preferred_element_type=jnp.float32
    )
    return summed.astype(jnp.bfloat16)


def on_device(alignment, gain_attn, w_proj, w_out, gain_head, w_head, masked, labels):
    weights = masked.reshape(-1).astype(jnp.float32)
    local_count = jnp.sum(weights)
    local_rows, single_block, segment, features = alignment.shape
    seq_devices = lax.axis_size("seq")
    split_view = alignment.reshape(local_rows, seq_devices, segment // seq_devices, features)
    column_block = lax.all_to_all(split_view, "seq", split_axis=1, concat_axis=0, tiled=True)
    seq_total, single, col_count, features = column_block.shape
    by_column = jnp.transpose(column_block.reshape(seq_total, col_count, features), (1, 0, 2))
    flat_rows = by_column.reshape(col_count * seq_total, features)
    projected = project(flat_rows, gain_attn, w_proj).reshape(
        col_count, seq_total, 4, HEADS, HEAD_DIM
    )

    def per_column(picked):
        weighted, totals = column_attention(picked[:, 0], picked[:, 1], picked[:, 2])
        attended = weighted / totals.T[:, :, None]
        gated_col = attended * jax.nn.sigmoid(picked[:, 3].astype(jnp.float32))
        return gated_col.reshape(seq_total, features).astype(jnp.bfloat16)

    gated = lax.map(per_column, projected).reshape(col_count * seq_total, features)
    result = finish(flat_rows, gated, w_out).reshape(col_count, seq_total, features)
    result = jnp.transpose(result, (1, 0, 2)).reshape(seq_total, single, col_count, features)
    updated = lax.all_to_all(result, "res", split_axis=0, concat_axis=1, tiled=True)
    features = updated.shape[3]
    flat_out = updated.reshape(-1, features)
    head_in = normalize(flat_out.astype(jnp.float32), gain_head).astype(jnp.bfloat16)
    logits = jnp.einsum("rc,ck->kr", head_in, w_head, preferred_element_type=jnp.float32)
    log_total = jnp.log(jnp.sum(jnp.exp(logits), axis=0))
    classes = jnp.arange(logits.shape[0], dtype=jnp.int32)[:, None]
    picked = jnp.sum(jnp.where(classes == labels.reshape(1, -1), logits, 0.0), axis=0)
    errors = log_total - picked
    local_loss = jnp.sum(errors * weights)
    loss_sum, mask_count = lax.psum((local_loss, local_count), ("seq", "res"))
    entries = flat_out.shape[0] * lax.axis_size("seq") * lax.axis_size("res")
    masked_loss = loss_sum / (1.0 + mask_count)
    mask_share = mask_count / entries
    return (updated, masked_loss, mask_share)


def solution(mesh):
    in_specs = (
        P("seq", "res", None, None),
        P(),
        P(),
        P(),
        P(),
        P(),
        P("res", None, "seq"),
        P("res", None, "seq"),
    )
    out_specs = (P("res", None, "seq", None), P(), P())
    return jax.shard_map(
        on_device, mesh=mesh, in_specs=in_specs, out_specs=out_specs, check_vma=False
    )
```

profile of v0, /device:TPU:12, one launch (start us, length us, event | category | flops | bytes accessed | tf_op | source)
XLA Modules:
  0.0 152.1 jit_solution(10787070603162363327)
XLA Ops:
  0.7 2.4 %copy.61 = bf16[16,8,16,256]{3,2,0,1:T(8,128)(2,1)} copy(bf16[16,8,16,256]{3,2,1,0:T(8,128)(2,1)} %bitcast.113) | data formatting | bytes 2097152 | tf_op jit(solution)/shard_map/reshape | solution.py:50
  3.0 6.3 %all-to-all-start = ((bf16[16,8,16,256]{3,2,0,1:T(8,128)(2,1)}), bf16[16,8,16,256]{3,2,0,1:T(8,128)(2,1)S(1)}, u32[]{:S(2)}, u32[]{:S(2)}) async-start(bf16[16,8,16,256]{3,2,0,1:T(8,128)(2,1)} %copy.61), calls=%async_computation | async-start | bytes 2097152 | tf_op jit(solution)/shard_map/all_to_all | solution.py:51
  9.4 23.3 %all-to-all-done = bf16[16,8,16,256]{3,2,0,1:T(8,128)(2,1)S(1)} async-done(((bf16[16,8,16,256]{3,2,0,1:T(8,128)(2,1)}), bf16[16,8,16,256]{3,2,0,1:T(8,128)(2,1)S(1)}, u32[]{:S(2)}, u32[]{:S(2)}) %all-to-all-start) | async-done | bytes 1048608 | tf_op jit(solution)/shard_map/all_to_all | solution.py:51
  32.6 0.3 bitcast_convert_fusion
  32.9 1.2 bitcast_reduce_fusion
  34.1 1.2 copy.62
  35.3 1.6 %multiply_reduce_fusion.1 = f32[16,128]{1,0:T(8,128)S(1)} fusion(f32[16,128]{1,0:T(8,128)S(1)} %broadcast_multiply_fusion.1, f32[128,16,256]{2,1,0:T(8,128)S(1)} %bitcast.100), kind=kLoop, calls=%fused_computation.24 | loop fusion | flops 1570816 | bytes 2113536 | tf_op jit(solution)/shard_map/reduce_sum | solution.py:13
  37.0 1.4 multiply_convert_fusion
  38.3 3.2 %convolution_convert_fusion = bf16[2048,1024]{1,0:T(8,128)(2,1)} fusion(bf16[2048,256]{1,0:T(8,128)(2,1)S(1)} %bitcast.109, bf16[256,1024]{1,0:T(8,128)(2,1)S(1)} %bitcast.111), kind=kOutput, calls=%fused_computation.12 | convolution fusion | flops 1075838976 | bytes 5767168 | tf_op jit(solution)/shard_map/dot_general | solution.py:20
  41.5 6.5 %copy.63 = bf16[2048,1024]{0,1:T(8,128)(2,1)} copy(bf16[2048,1024]{1,0:T(8,128)(2,1)} %convolution_convert_fusion) | data formatting | bytes 8388608 | tf_op jit(solution)/shard_map/convert_element_type | solution.py:22
  48.0 3.6 %copy.80 = bf16[128,8,16,128]{3,2,1,0:T(8,128)(2,1)S(1)} copy(bf16[128,8,16,128]{3,1,2,0:T(8,128)(2,1)} %bitcast.106) | data formatting | bytes 8388608
  51.6 3.0 %copy.64 = bf16[16,128,4,8,32]{1,4,3,2,0:T(8,128)(2,1)} copy(bf16[16,128,4,8,32]{1,0,4,3,2:T(8,128)(2,1)S(1)} %bitcast.107) | data formatting | bytes 8388608 | tf_op jit(solution)/shard_map/while | solution.py:65
  54.7 26.1 %while.10 = (s32[]{:T(128)}, bf16[16,128,256]{2,1,0:T(8,128)(2,1)S(1)}, bf16[16,128,4,8,32]{1,4,3,2,0:T(8,128)(2,1)}, s32[]{:T(128)}) while((s32[]{:T(128)}, bf16[16,128,256]{2,1,0:T(8,128)(2,1)S(1)}, bf16[16,128,4,8,32]{1,4,3,2,0:T(8,128)(2,1)}, s32[]{:T(128)}) %tuple.42), condition=%wide.region_4.0_spmd, body=%wide.region_2.4_spmd.sunk | while | flops 17398784 | bytes 1646653 | solution.py:65
  54.7 1.0 dynamic-slice_bitcast_fusion.2
  55.6 0.3 fusion.21
  56.3 1.0 dynamic-slice_bitcast_fusion.2
  57.3 0.3 fusion.21
  57.9 1.0 dynamic-slice_bitcast_fusion.2
  58.9 0.3 fusion.21
  59.6 1.0 dynamic-slice_bitcast_fusion.2
  60.5 0.3 fusion.21
  60.9 0.2 fusion.22
  61.2 1.0 dynamic-slice_bitcast_fusion.2
  62.2 0.3 fusion.21
  62.8 1.0 dynamic-slice_bitcast_fusion.2
  63.8 0.3 fusion.21
  64.1 0.2 fusion.22
  64.5 1.0 dynamic-slice_bitcast_fusion.2
  65.4 0.3 fusion.21
  65.8 0.2 fusion.22
  66.1 1.0 dynamic-slice_bitcast_fusion.2
  67.1 0.3 fusion.21
  67.4 0.2 fusion.22
  67.7 1.0 dynamic-slice_bitcast_fusion.2
  68.7 0.3 fusion.21
  69.4 1.0 dynamic-slice_bitcast_fusion.2
  70.3 0.3 fusion.21
  70.7 0.2 fusion.22
  71.0 1.0 dynamic-slice_bitcast_fusion.2
  72.0 0.3 fusion.21
  72.6 1.0 dynamic-slice_bitcast_fusion.2
  73.6 0.3 fusion.21
  74.3 1.0 dynamic-slice_bitcast_fusion.2
  75.2 0.3 fusion.21
  75.9 1.0 dynamic-slice_bitcast_fusion.2
  76.9 0.3 fusion.21
  77.2 0.2 fusion.22
  77.5 1.0 dynamic-slice_bitcast_fusion.2
  78.5 0.3 fusion.21
  78.8 0.2 fusion.22
  79.2 1.0 dynamic-slice_bitcast_fusion.2
  80.2 0.3 fusion.21
  80.8 0.4 fusion.5
  81.3 1.6 %copy.85 = bf16[16,128,256]{2,0,1:T(8,128)(2,1)} copy(bf16[16,128,256]{2,1,0:T(8,128)(2,1)S(1)} %bitcast.110) | data formatting | bytes 2097152 | tf_op jit(solution)/shard_map/reshape | solution.py:66
  82.8 4.0 %all-to-all-start.1 = ((bf16[128,1,16,256]{3,2,1,0:T(8,128)(2,1)}), bf16[128,1,16,256]{3,2,1,0:T(8,128)(2,1)S(1)}, u32[]{:S(2)}, u32[]{:S(2)}) async-start(bf16[128,1,16,256]{3,2,1,0:T(8,128)(2,1)} %bitcast.79), calls=%async_computation.1 | async-start | bytes 2097152 | tf_op jit(solution)/shard_map/all_to_all | solution.py:68
  87.1 12.5 %all-to-all-done.1 = bf16[128,1,16,256]{3,2,1,0:T(8,128)(2,1)S(1)} async-done(((bf16[128,1,16,256]{3,2,1,0:T(8,128)(2,1)}), bf16[128,1,16,256]{3,2,1,0:T(8,128)(2,1)S(1)}, u32[]{:S(2)}, u32[]{:S(2)}) %all-to-all-start.1) | async-done | bytes 1048608 | tf_op jit(solution)/shard_map/all_to_all | solution.py:68
  99.6 0.3 convert_reduce_fusion
  100.3 0.3 copy.67
  100.5 0.7 multiply_reduce_fusion
  101.6 0.9 fusion.8
  102.5 1.1 exponential_reduce_fusion
  103.7 0.7 convert_reduce_fusion.1
  104.4 42.4 %all-reduce = (f32[]{:T(128)}, f32[]{:T(128)}) all-reduce(f32[]{:T(128)} %get-tuple-element.57, f32[]{:T(128)} %get-tuple-element.56), channel_id=1, replica_groups=mesh['seq'=8,'res'=4] {'seq','res'}, use_global_device_ids=true, to_apply=%region_10.11 | all-reduce | flops 2 | bytes 16 | tf_op jit(solution)/shard_map/psum | solution.py:78
  148.1 1.1 copy.75
  (73 shorter events, 4.8 us)
Async XLA Ops:
  0.6 80.2 %copy-start = (bf16[256,256]{1,0:T(8,128)(2,1)S(1)}, bf16[256,256]{1,0:T(8,128)(2,1)}, u32[]{:S(2)}) copy-start(bf16[256,256]{1,0:T(8,128)(2,1)} %param.13) | copy-start | bytes 393220
  0.6 8.6 %copy-start.2 = (bf16[256,4,256]{2,1,0:T(4,128)(2,1)S(1)}, bf16[256,4,256]{2,1,0:T(4,128)(2,1)}, u32[]{:S(2)}) copy-start(bf16[256,4,256]{2,1,0:T(4,128)(2,1)} %param.12) | copy-start | bytes 1572868
  3.0 29.6 %all-to-all-start = ((bf16[16,8,16,256]{3,2,0,1:T(8,128)(2,1)}), bf16[16,8,16,256]{3,2,0,1:T(8,128)(2,1)S(1)}, u32[]{:S(2)}, u32[]{:S(2)}) async-start(bf16[16,8,16,256]{3,2,0,1:T(8,128)(2,1)} %copy.61), calls=%async_computation | async-start | bytes 2097152 | tf_op jit(solution)/shard_map/all_to_all | solution.py:51
  35.3 1.7 %copy-start.5 = (f32[256]{0:T(256)S(1)}, f32[256]{0:T(256)}, u32[]{:S(2)}) copy-start(f32[256]{0:T(256)} %param.11) | copy-start | bytes 3076
  51.6 3.0 %copy-start.1 = (bf16[16,128,256]{2,1,0:T(8,128)(2,1)S(1)}, bf16[16,128,256]{2,1,0:T(8,128)(2,1)}, u32[]{:S(2)}) copy-start(bf16[16,128,256]{2,1,0:T(8,128)(2,1)} %custom-call) | copy-start | bytes 3145732
  81.3 5.6 %copy-start.3 = (s32[32,4,16]{0,2,1:T(8,128)S(1)}, s32[32,4,16]{0,2,1:T(8,128)}, u32[]{:S(2)}) copy-start(s32[32,4,16]{0,2,1:T(8,128)} %param.17) | copy-start | bytes 24580
  81.3 5.7 %copy-start.4 = (s32[32,4,16]{0,2,1:T(8,128)S(1)}, s32[32,4,16]{0,2,1:T(8,128)}, u32[]{:S(2)}) copy-start(s32[32,4,16]{0,2,1:T(8,128)} %param.16) | copy-start | bytes 24580
  82.8 16.8 %all-to-all-start.1 = ((bf16[128,1,16,256]{3,2,1,0:T(8,128)(2,1)}), bf16[128,1,16,256]{3,2,1,0:T(8,128)(2,1)S(1)}, u32[]{:S(2)}, u32[]{:S(2)}) async-start(bf16[128,1,16,256]{3,2,1,0:T(8,128)(2,1)} %bitcast.79), calls=%async_computation.1 | async-start | bytes 2097152 | tf_op jit(solution)/shard_map/all_to_all | solution.py:68
  100.2 1.4 copy-start.6
where the time goes:
time: 153 us; the launch traced here: 152 us
  blocking collectives  42.4 us (28%)
  local copies, waits for them, and re-layouts  38.2 us (25%)
  waiting for transfers between devices  35.8 us (23%)
  matrix products  12.7 us (8%)
  starting transfers between devices  10.2 us (7%)
  other arithmetic  7 us (5%)
  between operations  5.09 us (3%)
    psum x1, blocking collectives, on_device(): loss_sum, mask_count = lax.psum((local_loss, local_count), ('seq', 'res'))  42.4 us
    all_to_all x1, waiting for transfers between devices, on_device(): lax.all_to_all(split_view, 'seq', split_axis=1, concat_axis=0, tiled=True)  23.3 us
    squeeze x16, local copies, waits for them, and re-layouts, on_device(): lax.map(per_column, projected).reshape(col_count * seq_total, features)  15.5 us
    all_to_all x1, waiting for transfers between devices, on_device(): lax.all_to_all(result, 'res', split_axis=0, concat_axis=1, tiled=True)  12.5 us
    convert_element_type x1, local copies, waits for them, and re-layouts, project(): return jnp.dot(normed, w_proj.reshape(features, 4 * features), preferred_...  6.52 us
    all_to_all x1, starting transfers between devices, on_device(): lax.all_to_all(split_view, 'seq', split_axis=1, concat_axis=0, tiled=True)  6.25 us
    dot_general x16, matrix products, column_attention(): jnp.einsum('shd,thd->hst', queries, key_part, preferred_element_type=jnp....  5.03 us
    unnamed x19, local copies, waits for them, and re-layouts  4.99 us
  transfers between devices with their start and end apart: 2, of which 2 were waited for; matrix products, arithmetic and copies ran while one was open for 0% of the time, Pallas kernels for 0%

commit v1 on v0

--- a/solution.py
+++ b/solution.py
@@ -75,7 +75,7 @@
     picked = jnp.sum(jnp.where(classes == labels.reshape(1, -1), logits, 0.0), axis=0)
     errors = log_total - picked
     local_loss = jnp.sum(errors * weights)
-    loss_sum, mask_count = lax.psum((local_loss, local_count), ("seq", "res"))
+    loss_sum, mask_count = lax.psum(lax.psum((local_loss, local_count), "res"), "seq")
     entries = flat_out.shape[0] * lax.axis_size("seq") * lax.axis_size("res")
     masked_loss = loss_sum / (1.0 + mask_count)
     mask_share = mask_count / entries

time: 153 us -> 142 us (0.928)
  the two profiles are of different devices: /device:TPU:12 before, /device:TPU:0 now
where the time goes in v1:
time: 142 us; the launch traced here: 141 us
  waiting for transfers between devices  39.6 us (28%)
  local copies, waits for them, and re-layouts  38.2 us (27%)
  blocking collectives  26.4 us (19%)
  matrix products  12.7 us (9%)
  starting transfers between devices  11 us (8%)
  other arithmetic  7 us (5%)
  between operations  5.11 us (4%)
    all_to_all x1, waiting for transfers between devices, on_device(): lax.all_to_all(split_view, 'seq', split_axis=1, concat_axis=0, tiled=True)  25.7 us
    psum x1, blocking collectives, on_device(): lax.psum(lax.psum((local_loss, local_count), 'res'), 'seq')  20.1 us
    squeeze x16, local copies, waits for them, and re-layouts, on_device(): lax.map(per_column, projected).reshape(col_count * seq_total, features)  15.5 us
    all_to_all x1, waiting for transfers between devices, on_device(): lax.all_to_all(result, 'res', split_axis=0, concat_axis=1, tiled=True)  13.9 us
    all_to_all x1, starting transfers between devices, on_device(): lax.all_to_all(split_view, 'seq', split_axis=1, concat_axis=0, tiled=True)  7.28 us
    convert_element_type x1, local copies, waits for them, and re-layouts, project(): return jnp.dot(normed, w_proj.reshape(features, 4 * features), preferred_...  6.52 us
    psum x1, blocking collectives, on_device(): lax.psum((local_loss, local_count), 'res')  6.37 us
    dot_general x16, matrix products, column_attention(): jnp.einsum('shd,thd->hst', queries, key_part, preferred_element_type=jnp....  5.03 us
  transfers between devices with their start and end apart: 2, of which 2 were waited for; matrix products, arithmetic and copies ran while one was open for 0% of the time, Pallas kernels for 0%

profile of v1, /device:TPU:0, one launch (start us, length us, event | category | flops | bytes accessed | tf_op | source)
XLA Modules:
  0.0 140.7 jit_solution(9995308563212275326)
XLA Ops:
  0.7 2.4 %copy.61 = bf16[16,8,16,256]{3,2,0,1:T(8,128)(2,1)} copy(bf16[16,8,16,256]{3,2,1,0:T(8,128)(2,1)} %bitcast.113) | data formatting | bytes 2097152 | tf_op jit(solution)/shard_map/reshape | solution.py:50
  3.0 7.3 %all-to-all-start = ((bf16[16,8,16,256]{3,2,0,1:T(8,128)(2,1)}), bf16[16,8,16,256]{3,2,0,1:T(8,128)(2,1)S(1)}, u32[]{:S(2)}, u32[]{:S(2)}) async-start(bf16[16,8,16,256]{3,2,0,1:T(8,128)(2,1)} %copy.61), calls=%async_computation | async-start | bytes 2097152 | tf_op jit(solution)/shard_map/all_to_all | solution.py:51
  10.4 25.7 %all-to-all-done = bf16[16,8,16,256]{3,2,0,1:T(8,128)(2,1)S(1)} async-done(((bf16[16,8,16,256]{3,2,0,1:T(8,128)(2,1)}), bf16[16,8,16,256]{3,2,0,1:T(8,128)(2,1)S(1)}, u32[]{:S(2)}, u32[]{:S(2)}) %all-to-all-start) | async-done | bytes 1048608 | tf_op jit(solution)/shard_map/all_to_all | solution.py:51
  36.1 0.3 bitcast_convert_fusion
  36.3 1.2 bitcast_reduce_fusion
  37.5 1.2 copy.62
  38.8 1.6 %multiply_reduce_fusion.1 = f32[16,128]{1,0:T(8,128)S(1)} fusion(f32[16,128]{1,0:T(8,128)S(1)} %broadcast_multiply_fusion.1, f32[128,16,256]{2,1,0:T(8,128)S(1)} %bitcast.100), kind=kLoop, calls=%fused_computation.24 | loop fusion | flops 1570816 | bytes 2113536 | tf_op jit(solution)/shard_map/reduce_sum | solution.py:13
  40.4 1.4 multiply_convert_fusion
  41.8 3.2 %convolution_convert_fusion = bf16[2048,1024]{1,0:T(8,128)(2,1)} fusion(bf16[2048,256]{1,0:T(8,128)(2,1)S(1)} %bitcast.109, bf16[256,1024]{1,0:T(8,128)(2,1)S(1)} %bitcast.111), kind=kOutput, calls=%fused_computation.12 | convolution fusion | flops 1075838976 | bytes 5767168 | tf_op jit(solution)/shard_map/dot_general | solution.py:20
  45.0 6.5 %copy.63 = bf16[2048,1024]{0,1:T(8,128)(2,1)} copy(bf16[2048,1024]{1,0:T(8,128)(2,1)} %convolution_convert_fusion) | data formatting | bytes 8388608 | tf_op jit(solution)/shard_map/convert_element_type | solution.py:22
  51.5 3.6 %copy.80 = bf16[128,8,16,128]{3,2,1,0:T(8,128)(2,1)S(1)} copy(bf16[128,8,16,128]{3,1,2,0:T(8,128)(2,1)} %bitcast.106) | data formatting | bytes 8388608
  55.1 3.0 %copy.64 = bf16[16,128,4,8,32]{1,4,3,2,0:T(8,128)(2,1)} copy(bf16[16,128,4,8,32]{1,0,4,3,2:T(8,128)(2,1)S(1)} %bitcast.107) | data formatting | bytes 8388608 | tf_op jit(solution)/shard_map/while | solution.py:65
  58.1 26.1 %while.10 = (s32[]{:T(128)}, bf16[16,128,256]{2,1,0:T(8,128)(2,1)S(1)}, bf16[16,128,4,8,32]{1,4,3,2,0:T(8,128)(2,1)}, s32[]{:T(128)}) while((s32[]{:T(128)}, bf16[16,128,256]{2,1,0:T(8,128)(2,1)S(1)}, bf16[16,128,4,8,32]{1,4,3,2,0:T(8,128)(2,1)}, s32[]{:T(128)}) %tuple.42), condition=%wide.region_4.0_spmd, body=%wide.region_2.4_spmd.sunk | while | flops 17398784 | bytes 1646653 | solution.py:65
  58.1 1.0 dynamic-slice_bitcast_fusion.2
  59.1 0.3 fusion.21
  59.7 1.0 dynamic-slice_bitcast_fusion.2
  60.7 0.3 fusion.21
  61.0 0.2 fusion.22
  61.4 1.0 dynamic-slice_bitcast_fusion.2
  62.3 0.3 fusion.21
  63.0 1.0 dynamic-slice_bitcast_fusion.2
  64.0 0.3 fusion.21
  64.6 1.0 dynamic-slice_bitcast_fusion.2
  65.6 0.3 fusion.21
  65.9 0.2 fusion.22
  66.3 1.0 dynamic-slice_bitcast_fusion.2
  67.2 0.3 fusion.21
  67.6 0.2 fusion.22
  67.9 1.0 dynamic-slice_bitcast_fusion.2
  68.9 0.3 fusion.21
  69.2 0.2 fusion.22
  69.5 1.0 dynamic-slice_bitcast_fusion.2
  70.5 0.3 fusion.21
  71.2 1.0 dynamic-slice_bitcast_fusion.2
  72.1 0.3 fusion.21
  72.8 1.0 dynamic-slice_bitcast_fusion.2
  73.8 0.3 fusion.21
  74.4 1.0 dynamic-slice_bitcast_fusion.2
  75.4 0.3 fusion.21
  76.1 1.0 dynamic-slice_bitcast_fusion.2
  77.1 0.3 fusion.21
  77.7 1.0 dynamic-slice_bitcast_fusion.2
  78.7 0.3 fusion.21
  79.0 0.2 fusion.22
  79.3 1.0 dynamic-slice_bitcast_fusion.2
  80.3 0.3 fusion.21
  81.0 1.0 dynamic-slice_bitcast_fusion.2
  82.0 0.3 fusion.21
  82.3 0.2 fusion.22
  82.6 1.0 dynamic-slice_bitcast_fusion.2
  83.6 0.3 fusion.21
  84.3 0.4 fusion.5
  84.7 1.6 %copy.85 = bf16[16,128,256]{2,0,1:T(8,128)(2,1)} copy(bf16[16,128,256]{2,1,0:T(8,128)(2,1)S(1)} %bitcast.110) | data formatting | bytes 2097152 | tf_op jit(solution)/shard_map/reshape | solution.py:66
  86.3 3.7 %all-to-all-start.1 = ((bf16[128,1,16,256]{3,2,1,0:T(8,128)(2,1)}), bf16[128,1,16,256]{3,2,1,0:T(8,128)(2,1)S(1)}, u32[]{:S(2)}, u32[]{:S(2)}) async-start(bf16[128,1,16,256]{3,2,1,0:T(8,128)(2,1)} %bitcast.79), calls=%async_computation.1 | async-start | bytes 2097152 | tf_op jit(solution)/shard_map/all_to_all | solution.py:68
  90.3 13.9 %all-to-all-done.1 = bf16[128,1,16,256]{3,2,1,0:T(8,128)(2,1)S(1)} async-done(((bf16[128,1,16,256]{3,2,1,0:T(8,128)(2,1)}), bf16[128,1,16,256]{3,2,1,0:T(8,128)(2,1)S(1)}, u32[]{:S(2)}, u32[]{:S(2)}) %all-to-all-start.1) | async-done | bytes 1048608 | tf_op jit(solution)/shard_map/all_to_all | solution.py:68
  104.2 0.3 convert_reduce_fusion
  104.8 0.3 copy.67
  105.1 0.7 multiply_reduce_fusion
  106.2 0.9 fusion.8
  107.1 1.1 exponential_reduce_fusion
  108.3 0.7 convert_reduce_fusion.1
  109.0 6.4 %all-reduce.1 = (f32[]{:T(128)}, f32[]{:T(128)}) all-reduce(f32[]{:T(128)} %get-tuple-element.57, f32[]{:T(128)} %get-tuple-element.56), channel_id=1, replica_groups=mesh['seq'=8,'res'=4] {'res'}, use_global_device_ids=true, to_apply=%region_10.11 | all-reduce | flops 2 | bytes 16 | tf_op jit(solution)/shard_map/psum | solution.py:78
  115.3 20.1 %all-reduce = (f32[]{:T(128)}, f32[]{:T(128)}) all-reduce(f32[]{:T(128)} %get-tuple-element.66, f32[]{:T(128)} %get-tuple-element.67), channel_id=1, replica_groups=mesh['seq'=8,'res'=4] {'seq'}, use_global_device_ids=true, to_apply=%region_11.12 | all-reduce | flops 2 | bytes 16 | tf_op jit(solution)/shard_map/psum | solution.py:78
  136.7 1.1 copy.75
  (74 shorter events, 5.0 us)
Async XLA Ops:
  0.6 83.6 %copy-start = (bf16[256,256]{1,0:T(8,128)(2,1)S(1)}, bf16[256,256]{1,0:T(8,128)(2,1)}, u32[]{:S(2)}) copy-start(bf16[256,256]{1,0:T(8,128)(2,1)} %param.13) | copy-start | bytes 393220
  0.6 9.7 %copy-start.2 = (bf16[256,4,256]{2,1,0:T(4,128)(2,1)S(1)}, bf16[256,4,256]{2,1,0:T(4,128)(2,1)}, u32[]{:S(2)}) copy-start(bf16[256,4,256]{2,1,0:T(4,128)(2,1)} %param.12) | copy-start | bytes 1572868
  3.0 33.0 %all-to-all-start = ((bf16[16,8,16,256]{3,2,0,1:T(8,128)(2,1)}), bf16[16,8,16,256]{3,2,0,1:T(8,128)(2,1)S(1)}, u32[]{:S(2)}, u32[]{:S(2)}) async-start(bf16[16,8,16,256]{3,2,0,1:T(8,128)(2,1)} %copy.61), calls=%async_computation | async-start | bytes 2097152 | tf_op jit(solution)/shard_map/all_to_all | solution.py:51
  38.7 1.7 %copy-start.5 = (f32[256]{0:T(256)S(1)}, f32[256]{0:T(256)}, u32[]{:S(2)}) copy-start(f32[256]{0:T(256)} %param.11) | copy-start | bytes 3076
  55.1 3.0 %copy-start.1 = (bf16[16,128,256]{2,1,0:T(8,128)(2,1)S(1)}, bf16[16,128,256]{2,1,0:T(8,128)(2,1)}, u32[]{:S(2)}) copy-start(bf16[16,128,256]{2,1,0:T(8,128)(2,1)} %custom-call) | copy-start | bytes 3145732
  84.7 5.3 %copy-start.3 = (s32[32,4,16]{0,2,1:T(8,128)S(1)}, s32[32,4,16]{0,2,1:T(8,128)}, u32[]{:S(2)}) copy-start(s32[32,4,16]{0,2,1:T(8,128)} %param.17) | copy-start | bytes 24580
  84.7 5.5 %copy-start.4 = (s32[32,4,16]{0,2,1:T(8,128)S(1)}, s32[32,4,16]{0,2,1:T(8,128)}, u32[]{:S(2)}) copy-start(s32[32,4,16]{0,2,1:T(8,128)} %param.16) | copy-start | bytes 24580
  86.3 17.9 %all-to-all-start.1 = ((bf16[128,1,16,256]{3,2,1,0:T(8,128)(2,1)}), bf16[128,1,16,256]{3,2,1,0:T(8,128)(2,1)S(1)}, u32[]{:S(2)}, u32[]{:S(2)}) async-start(bf16[128,1,16,256]{3,2,1,0:T(8,128)(2,1)} %bitcast.79), calls=%async_computation.1 | async-start | bytes 2097152 | tf_op jit(solution)/shard_map/all_to_all | solution.py:68
  104.8 1.4 copy-start.6
